TPU v7x, 32 devices: a whole 2x2x4 slice. The times are simulated.
32 devices in a mesh: row: 8 (over y, x, core), col: 4 (over z).
Axes of the slice: x: 2, y: 2, z: 4, core: 2. Of those that a mesh axis runs over, the one named last changes fastest.
Arguments:
- tiles: bfloat16 [16384, 128, 128], P(('row', 'col'))
- row_tiles: int32 [16384], P(('row', 'col')), may hold values from 0 to 127, as said below
- col_tiles: int32 [16384], P(('row', 'col')), may hold values from 0 to 1023, as said below
- counts: int32 [32], P(('row', 'col')), may hold values from 128 to 512, as said below
- right_basis: float32 [100, 131072], P(None, ('row', 'col'))
- left_basis: float32 [100, 131072], P(None, ('row', 'col'))
- start: float32 [131072], P(('row', 'col'))
Outputs:
- left_vectors: float32 [2, 131072], P(None, ('row', 'col'))
- right_vectors: float32 [2, 131072], P(None, ('row', 'col'))
- coefficients: float32 [5], replicated
Inputs may be any that keep to these rules, and one draw needn't show every extreme that they name: `row_tiles`: tile rows lie within a row group. `col_tiles`: device d owns tile columns d * 32 up to (d + 1) * 32 - 1. The 512 slots of one device name at most 8 distinct tile columns owned by any one device; in every draw some owner receives exactly 8 distinct live tile columns from every device. `counts`: slots at or beyond a block's count hold no part of the matrix; in every draw some block has 512 live slots.
All inputs are finite; a program needn't handle non-finite values.
Results may differ from a plain program's by a relative error of at most 0.0045.
The roundings to bfloat16 on the way count: a program that leaves them out, or rounds other values in their place, can miss the bound.
Values may be sent and summed in bfloat16 or wider, within the bound.
A program may use at most 128 MiB of HBM per device.

v0:
```python
import functools

import jax
import jax.numpy as jnp
from jax import lax
from jax.experimental import pallas as pl
from jax.experimental.pallas import tpu as pltpu
from jax.sharding import PartitionSpec as P

PEER_TILES = 8
GROUP = 16
UNROLL = 8
CHUNKS = 8
MESH = pl.DeviceIdType.MESH
F32 = jnp.float32
BF16 = jnp.bfloat16


def hot(condition):
    return jnp.where(condition, 1.0, 0.0).astype(BF16)


def dot(left, right):
    return jnp.dot(left, right, preferred_element_type=F32)


def exact_dot(selector, values):
    high = values.astype(BF16)
    rest = values - high.astype(F32)
    middle = rest.astype(BF16)
    low = (rest - middle.astype(F32)).astype(BF16)
    return dot(selector, high) + (dot(selector, middle) + dot(selector, low))


def kernel(
    n_row, n_col, row_total,
    tiles_hbm, row_line, col_line, counts_ref, right_ref, left_hbm, start_ref,
    lefts_ref, rights_ref, coeffs_ref,
    tiles, left_ref, place_buf, c_buf, n_buf, pack, xbuf, outgoing, abuf, ypart, rsbuf, agbuf,
    r_ref, rem_right, right_one, left_one, acc_ref, x_gathered, products,
    tile_sems, left_sem, send_sems, recv_sems,
):
    devices = n_row * n_col
    my_row = lax.axis_index("row")
    my_col = lax.axis_index("col")
    me = my_row * n_col + my_col
    slots, size = tiles.shape[0], tiles.shape[1]
    per_owner = start_ref.shape[0]
    group_tiles = per_owner * n_col
    table = devices * PEER_TILES
    basis_rows = right_ref.shape[0]

    chunk = slots // CHUNKS
    tile_copies = [
        pltpu.make_async_copy(
            tiles_hbm.at[pl.ds(i * chunk, chunk)], tiles.at[pl.ds(i * chunk, chunk)], tile_sems.at[i]
        )
        for i in range(CHUNKS)
    ]
    left_copy = pltpu.make_async_copy(left_hbm, left_ref, left_sem)
    left_copy.start()
    for copy in tile_copies:
        copy.start()

    barrier = pltpu.get_barrier_semaphore()

    peer_cols = [my_col] + [lax.rem(my_col + i, n_col) for i in range(1, n_col)]

    def greet(row, cols):
        for col in cols:
            pl.semaphore_signal(
                barrier, inc=1, device_id={"row": row, "col": col}, device_id_type=MESH
            )

    def greet_row(i, _):
        greet(lax.rem(my_row + i, n_row), peer_cols)
        return 0

    lax.fori_loop(1, n_row, greet_row, 0)
    greet(my_row, peer_cols[1:])

    phases = [0]

    def next_phase():
        phases[0] += 1
        return phases[0] - 1

    pending = []

    def send_all(source, buf):
        phase = next_phase()

        def send(row, col):
            pltpu.make_async_remote_copy(
                src_ref=source(row * n_col + col), dst_ref=buf.at[me],
                send_sem=send_sems.at[phase], recv_sem=recv_sems.at[phase],
                device_id={"row": row, "col": col}, device_id_type=MESH,
            ).start()

        def step(i, _):
            row = lax.rem(my_row + i, n_row)
            for col in peer_cols:
                send(row, col)
            return 0

        lax.fori_loop(1, n_row, step, 0)
        for col in peer_cols[1:]:
            send(my_row, col)
        many = buf.at[pl.ds(0, devices - 1)]
        pending.append((many, phase))
        return lambda: pltpu.make_async_copy(many, many, recv_sems.at[phase]).wait()

    def send_col(source, buf):
        phase = next_phase()
        for i in range(1, n_col):
            target = peer_cols[i]
            pltpu.make_async_remote_copy(
                src_ref=source(target), dst_ref=buf.at[my_col],
                send_sem=send_sems.at[phase], recv_sem=recv_sems.at[phase],
                device_id={"row": my_row, "col": target}, device_id_type=MESH,
            ).start()
        many = buf.at[pl.ds(0, n_col - 1)]
        pending.append((many, phase))
        return lambda: pltpu.make_async_copy(many, many, recv_sems.at[phase]).wait()

    def partial_coeffs(basis, x_ref, buf):
        total = jnp.zeros((basis_rows, size), F32)
        for k in range(per_owner):
            total = total + basis[:, k * size:(k + 1) * size] * x_ref[k:k + 1, :]
        acc_ref[0:basis_rows, :] = total
        buf[me] = jnp.sum(acc_ref[...].T, axis=0, keepdims=True)

    def remainder(basis, x_ref, out_ref, buf, norm_buf):
        line = jnp.sum(buf[...], axis=0) / row_total
        column = jnp.broadcast_to(line, (size, size)).T[0:basis_rows, :]
        for k in range(per_owner):
            part = jnp.sum(basis[:, k * size:(k + 1) * size] * column, axis=0, keepdims=True)
            out_ref[k:k + 1, :] = x_ref[k:k + 1, :] - part
        value = out_ref[...]
        norm_buf[me] = jnp.sum(value * value, axis=0, keepdims=True)

    def norm_of(norm_buf):
        line = jnp.sum(norm_buf[...], axis=0)
        return jnp.sqrt(jnp.sum(line, axis=1, keepdims=True) / row_total + 1e-06)

    def put_coeff(i, value):
        coeffs_ref[i:i + 1, :] = jnp.broadcast_to(value, (1, size))

    def put_rows(ref, row, value):
        for k in range(per_owner):
            ref[row:row + 1, k * size:(k + 1) * size] = value[k:k + 1, :]

    acc_ref[...] = jnp.zeros_like(acc_ref)
    partial_coeffs(right_ref, start_ref, c_buf.at[0])

    def upright(line):
        return jnp.broadcast_to(line.astype(F32), (size, slots)).T

    live_line = jnp.where(
        lax.broadcasted_iota(jnp.int32, (1, slots), 1) < counts_ref[0], row_line[...], -1
    )
    live_column = upright(live_line)[:, 0:1]
    columns = upright(col_line[...])[:, 0:1].astype(jnp.int32)
    owner = lax.div(columns, per_owner)
    place = lax.rem(columns, per_owner)
    owner_hot = hot(owner == lax.broadcasted_iota(jnp.int32, (slots, devices), 1))
    place_here = place == lax.broadcasted_iota(jnp.int32, (slots, size), 1)
    named = lax.dot_general(
        owner_hot, hot(place_here), (((0,), (0,)), ((), ())), preferred_element_type=F32
    )
    touched = named > 0.5
    earlier = hot(
        lax.broadcasted_iota(jnp.int32, (size, size), 0)
        <= lax.broadcasted_iota(jnp.int32, (size, size), 1)
    )
    rank = jnp.where(touched, dot(hot(touched), earlier) - 1.0, -1.0)
    for i in range(devices):
        pack[0, i, 0:1, :] = rank[i:i + 1, :]
    place_buf[me] = pack[0, me, 0:1, :]
    slot_rank = jnp.sum(
        jnp.where(place_here, dot(owner_hot, rank.astype(BF16)), 0.0), axis=1, keepdims=True
    )
    entry = owner.astype(F32) * PEER_TILES + slot_rank
    entry_hot = hot(entry == lax.broadcasted_iota(jnp.int32, (slots, table), 1).astype(F32))
    entry_line = jnp.broadcast_to(entry, (slots, size)).T[0:1, :]
    entry_hot_t = hot(entry_line == lax.broadcasted_iota(jnp.int32, (table, slots), 0).astype(F32))
    row_hot = hot(
        live_column == lax.broadcasted_iota(jnp.int32, (slots, group_tiles), 1).astype(F32)
    )
    row_hot_t = hot(live_line == lax.broadcasted_iota(jnp.int32, (group_tiles, slots), 0))

    pl.semaphore_wait(barrier, devices - 1)
    coeffs_in = send_all(lambda target: c_buf.at[0, me], c_buf.at[0])
    places_in = send_all(lambda target: pack.at[0, target, pl.ds(0, 1)], place_buf)
    places_in()
    spread = hot(
        lax.div(lax.broadcasted_iota(jnp.int32, (table, devices), 0), PEER_TILES)
        == lax.broadcasted_iota(jnp.int32, (table, devices), 1)
    )
    ranks = jnp.concatenate([place_buf[i] for i in range(devices)], axis=0).astype(BF16)
    wanted = lax.rem(lax.broadcasted_iota(jnp.int32, (table, size), 0), PEER_TILES).astype(F32)
    selector_all = jnp.where(dot(spread, ranks) == wanted, 1.0, 0.0)
    selector = selector_all[:, 0:per_owner].astype(BF16)
    selector_t = selector_all.T[0:per_owner, :].astype(BF16)

    def diagonal(wide):
        index = lax.broadcasted_iota(jnp.int32, (GROUP, size), 0)
        total = wide[:, 0:size]
        for k in range(1, GROUP):
            total = jnp.where(index == k, wide[:, k * size:(k + 1) * size], total)
        return total

    def tile_products(transposed):
        def one(first):
            vectors = x_gathered[pl.ds(first, GROUP), :]
            block = tiles[pl.ds(first, GROUP)]
            if transposed:
                joined = jnp.concatenate([block[k] for k in range(GROUP)], axis=1)
                wide = dot(vectors, joined)
            else:
                wide = lax.dot_general(
                    vectors, block.reshape(GROUP * size, size),
                    (((1,), (1,)), ((), ())), preferred_element_type=F32,
                )
            return diagonal(wide)

        def step(g, _):
            firsts = [
                pl.multiple_of(g * (GROUP * UNROLL) + h * GROUP, GROUP) for h in range(UNROLL)
            ]
            found = [one(first) for first in firsts]
            for first, value in zip(firsts, found):
                products[pl.ds(first, GROUP), :] = value
            return 0

        lax.fori_loop(0, slots // (GROUP * UNROLL), step, 0)

    def share_right(r_value, index, norm_buf):
        packed = exact_dot(selector, r_value)
        pack[index + 1] = packed.reshape(devices, PEER_TILES, size)
        norms_in = send_all(lambda target: norm_buf.at[me], norm_buf)
        values_in = send_all(lambda target: pack.at[index + 1, target], xbuf.at[index])
        xbuf[index, me] = pack[index + 1, me]
        norms_in()
        return values_in

    def rows_product(index, norm):
        values = xbuf[index].reshape(table, size)
        x_gathered[...] = dot(entry_hot, (values / norm).astype(BF16)).astype(BF16)
        tile_products(False)
        ypart[index] = exact_dot(row_hot_t, products[...]).reshape(n_col, per_owner, size)
        rows_in = send_col(lambda target: ypart.at[index, target], rsbuf.at[index])
        rsbuf[index, my_col] = ypart[index, my_col]
        rows_in()
        total = rsbuf[index, 0]
        for i in range(1, n_col):
            total = total + rsbuf[index, i]
        return total

    def share_left(index, norm_buf):
        norms_in = send_all(lambda target: norm_buf.at[me], norm_buf)
        agbuf[index, my_col] = rem_right[index]
        values_in = send_col(lambda target: rem_right.at[index], agbuf.at[index])
        norms_in()
        return values_in

    def columns_product(index, norm):
        values = agbuf[index].reshape(group_tiles, size)
        x_gathered[...] = dot(row_hot, (values / norm).astype(BF16)).astype(BF16)
        tile_products(True)
        outgoing[index] = exact_dot(entry_hot_t, products[...]).reshape(devices, PEER_TILES, size)
        sums_in = send_all(lambda target: outgoing.at[index, target], abuf.at[index])
        abuf[index, me] = outgoing[index, me]
        sums_in()
        return exact_dot(selector_t, abuf[index].reshape(table, size))

    def reduce_coeffs(basis, x_ref, index):
        partial_coeffs(basis, x_ref, c_buf.at[index])
        send_all(lambda target: c_buf.at[index, me], c_buf.at[index])()

    scratch = r_ref
    coeffs_in()
    remainder(right_ref, start_ref, scratch.at[1], c_buf.at[0], n_buf.at[0])
    values_in = share_right(scratch[1], 0, n_buf.at[0])
    norm = norm_of(n_buf.at[0])
    put_coeff(0, norm)
    right_one[...] = scratch[1] / norm
    values_in()
    for copy in tile_copies:
        copy.wait()
    scratch[0] = rows_product(0, norm)
    left_copy.wait()
    reduce_coeffs(left_ref, scratch.at[0], 1)
    remainder(left_ref, scratch.at[0], rem_right.at[0], c_buf.at[1], n_buf.at[1])
    values_in = share_left(0, n_buf.at[1])
    norm = norm_of(n_buf.at[1])
    put_coeff(1, norm)
    left_one[...] = rem_right[0] / norm
    put_rows(lefts_ref, 0, left_one)
    values_in()
    scratch[0] = columns_product(0, norm) - norm * right_one[...]
    reduce_coeffs(right_ref, scratch.at[0], 2)
    remainder(right_ref, scratch.at[0], scratch.at[1], c_buf.at[2], n_buf.at[2])
    values_in = share_right(scratch[1], 1, n_buf.at[2])
    norm = norm_of(n_buf.at[2])
    put_coeff(2, norm)
    right_one[...] = scratch[1] / norm
    put_rows(rights_ref, 0, right_one)
    values_in()
    scratch[0] = rows_product(1, norm) - norm * left_one[...]
    reduce_coeffs(left_ref, scratch.at[0], 3)
    remainder(left_ref, scratch.at[0], rem_right.at[1], c_buf.at[3], n_buf.at[3])
    values_in = share_left(1, n_buf.at[3])
    norm = norm_of(n_buf.at[3])
    put_coeff(3, norm)
    left_one[...] = rem_right[1] / norm
    put_rows(lefts_ref, 1, left_one)
    values_in()
    scratch[0] = columns_product(1, norm) - norm * right_one[...]
    reduce_coeffs(right_ref, scratch.at[0], 4)
    remainder(right_ref, scratch.at[0], scratch.at[1], c_buf.at[4], n_buf.at[4])
    send_all(lambda target: n_buf.at[4, me], n_buf.at[4])()
    norm = norm_of(n_buf.at[4])
    put_coeff(4, norm)
    right_one[...] = scratch[1] / norm
    put_rows(rights_ref, 1, right_one)

    for many, phase in pending:
        pltpu.make_async_copy(many, many, send_sems.at[phase]).wait()


def finish(lefts_in, rights_in, coeffs_in, lefts, rights, line):
    lefts[...] = lefts_in[...]
    rights[...] = rights_in[...]
    for i in range(5):
        line[i] = coeffs_in[i, 0]


def shards(tiles, row_tiles, col_tiles, counts, right_basis, left_basis, start):
    n_row, n_col = lax.axis_size("row"), lax.axis_size("col")
    devices = n_row * n_col
    slots, size = tiles.shape[0], tiles.shape[1]
    rows_dev = start.shape[0]
    per_owner = rows_dev // size
    row_total = float(rows_dev * devices)
    vmem = pl.BlockSpec(memory_space=pltpu.VMEM)
    hbm = pl.BlockSpec(memory_space=pl.ANY)
    n_phases = 20
    lefts, rights, coeffs = pl.pallas_call(
        functools.partial(kernel, n_row, n_col, row_total),
        out_shape=(
            jax.ShapeDtypeStruct((2, rows_dev), F32),
            jax.ShapeDtypeStruct((2, rows_dev), F32),
            jax.ShapeDtypeStruct((8, size), F32),
        ),
        in_specs=[
            hbm, vmem, vmem, pl.BlockSpec(memory_space=pltpu.SMEM), vmem, hbm, vmem
        ],
        out_specs=(vmem, vmem, vmem),
        scratch_shapes=[
            pltpu.VMEM(tiles.shape, BF16),
            pltpu.VMEM(left_basis.shape, F32),
            pltpu.VMEM((devices, 1, size), F32),
            pltpu.VMEM((5, devices, 1, size), F32),
            pltpu.VMEM((5, devices, 1, size), F32),
            pltpu.VMEM((3, devices, PEER_TILES, size), F32),
            pltpu.VMEM((2, devices, PEER_TILES, size), F32),
            pltpu.VMEM((2, devices, PEER_TILES, size), F32),
            pltpu.VMEM((2, devices, PEER_TILES, size), F32),
            pltpu.VMEM((2, n_col, per_owner, size), F32),
            pltpu.VMEM((2, n_col, per_owner, size), F32),
            pltpu.VMEM((2, n_col, per_owner, size), F32),
            pltpu.VMEM((2, per_owner, size), F32),
            pltpu.VMEM((2, per_owner, size), F32),
            pltpu.VMEM((per_owner, size), F32),
            pltpu.VMEM((per_owner, size), F32),
            pltpu.VMEM((size, size), F32),
            pltpu.VMEM((slots, size), BF16),
            pltpu.VMEM((slots, size), F32),
            pltpu.SemaphoreType.DMA((CHUNKS,)),
            pltpu.SemaphoreType.DMA,
            pltpu.SemaphoreType.DMA((n_phases,)),
            pltpu.SemaphoreType.DMA((n_phases,)),
        ],
        compiler_params=pltpu.CompilerParams(
            collective_id=0, has_side_effects=True, vmem_limit_bytes=60 * 1024 * 1024
        ),
    )(
        tiles, row_tiles.reshape(1, slots), col_tiles.reshape(1, slots), counts, right_basis, left_basis, start.reshape(per_owner, size),
    )
    lefts, rights, line = pl.pallas_call(
        finish,
        out_shape=(
            jax.ShapeDtypeStruct(lefts.shape, F32),
            jax.ShapeDtypeStruct(rights.shape, F32),
            jax.ShapeDtypeStruct((5,), F32),
        ),
        in_specs=[vmem, vmem, pl.BlockSpec(memory_space=pltpu.SMEM)],
        out_specs=(vmem, vmem, pl.BlockSpec(memory_space=pltpu.SMEM)),
    )(lefts, rights, coeffs)
    return lefts, rights, line


def solution(mesh):
    placed = (
        P(("row", "col"), None, None),
        P(("row", "col")),
        P(("row", "col")),
        P(("row", "col")),
        P(None, ("row", "col")),
        P(None, ("row", "col")),
        P(("row", "col")),
    )
    return jax.shard_map(
        shards,
        mesh=mesh,
        in_specs=placed,
        out_specs=(P(None, ("row", "col")), P(None, ("row", "col")), P()),
        check_vma=False,
    )
```

profile of v0, /device:TPU:0, one launch (start us, length us, event | category | flops | bytes accessed | tf_op | source)
XLA Modules:
  0.0 98.4 jit_solution(1892830687954206259)
XLA Ops:
  1.3 95.6 %shard_map.94 = (f32[2,4096]{1,0:T(2,128)}, f32[2,4096]{1,0:T(2,128)}, f32[8,128]{1,0:T(8,128)}) custom-call(bf16[512,128,128]{2,1,0:T(8,128)(2,1)} %tiles_hbm.1, s32[1,512]{1,0:T(1,128)} %bitcast.4, s32[1,512]{1,0:T(1,128)} %bitcast.5, s32[1]{0:T(128)S(6)} %copy.10.counts_ref, f32[100,4096]{1,0:T(8,128)} %right_ref.1, f32[100,4096]{1,0:T(8,128)} %left_hbm.1, ...), custom_call_target="tpu_custom_call" | custom-call | tf_op jit(solution)/shard_map/pallas_call | solution.py:349
  96.9 1.5 %shard_map.95 = (f32[2,4096]{1,0:T(2,128)}, f32[2,4096]{1,0:T(2,128)}, f32[5]{0:T(128)}) custom-call(f32[2,4096]{1,0:T(2,128)} %get-tuple-element.6.lefts_in, f32[2,4096]{1,0:T(2,128)} %get-tuple-element.7.rights_in, f32[8,128]{1,0:T(8,128)} %get-tuple-element.8.coeffs_in), custom_call_target="tpu_custom_call" | custom-call | tf_op jit(solution)/shard_map/pallas_call | solution.py:391
where the time goes:
time: 98.6 us; the launch traced here: 98.4 us
  Pallas kernels  97.1 us (98%)
  between operations  1.29 us (1%)
    pallas_call x1, Pallas kernels, shards(): pl.pallas_call(functools.partial(kernel, n_row, n_col, row_total), out_sh...  95.6 us

commit v1 on v0

v1 whole, which is shorter than its diff:
```python
import functools

import jax
import jax.numpy as jnp
from jax import lax
from jax.experimental import pallas as pl
from jax.experimental.pallas import tpu as pltpu
from jax.sharding import PartitionSpec as P

PEER_TILES = 8
GROUP = 16
UNROLL = 32
CHUNKS = 8
EARLY = 2
MESH = pl.DeviceIdType.MESH
F32 = jnp.float32
BF16 = jnp.bfloat16


def hot(condition):
    return jnp.where(condition, 1.0, 0.0).astype(BF16)


def dot(left, right):
    return jnp.dot(left, right, preferred_element_type=F32)


def exact_dot(selector, values):
    high = values.astype(BF16)
    rest = values - high.astype(F32)
    middle = rest.astype(BF16)
    low = (rest - middle.astype(F32)).astype(BF16)
    return dot(selector, high) + (dot(selector, middle) + dot(selector, low))


def kernel(
    n_row, n_col, row_total,
    tiles_hbm, rows_hbm, cols_hbm, counts_hbm, right_hbm, left_hbm, start_hbm,
    lefts_ref, rights_ref, coeffs_ref,
    tiles, flipped, left_ref, right_ref, row_line, col_line, counts_ref, start_ref,
    place_out, place_buf, c_buf, n_buf, pack_first, x_first, pack, xbuf, outgoing, abuf,
    ypart, rsbuf, share, agbuf, halves, gram_out, gram_in, gram_all,
    r_ref, right_one, left_one, acc_ref, x_gathered, products,
    tile_sems, input_sems, send_sems, recv_sems,
):
    devices = n_row * n_col
    my_row = lax.axis_index("row")
    my_col = lax.axis_index("col")
    me = my_row * n_col + my_col
    slots, size = tiles.shape[0], tiles.shape[1]
    per_owner = start_ref.shape[0]
    group_tiles = per_owner * n_col
    table = devices * PEER_TILES
    basis_rows = right_ref.shape[0]
    gram_rows = gram_out.shape[1]

    barrier = pltpu.get_barrier_semaphore()

    if n_col == 4:
        across = lax.rem(my_col + 2, n_col)
        other_cols = [n_col - 1 - my_col, across, n_col - 1 - across]
    else:
        other_cols = [lax.rem(my_col + i, n_col) for i in range(1, n_col)]

    def each_peer(act):
        for col in other_cols:
            def step(i, _, col=col):
                act(lax.rem(my_row + i, n_row), col)
                return 0

            lax.fori_loop(0, n_row, step, 0)

        def own_step(i, _):
            act(lax.rem(my_row + i, n_row), my_col)
            return 0

        lax.fori_loop(1, n_row, own_step, 0)

    each_peer(
        lambda row, col: pl.semaphore_signal(
            barrier, inc=1, device_id={"row": row, "col": col}, device_id_type=MESH
        )
    )

    small = [(start_hbm, start_ref), (rows_hbm, row_line), (cols_hbm, col_line), (counts_hbm, counts_ref)]
    small_copies = [
        pltpu.make_async_copy(source, target, input_sems.at[i])
        for i, (source, target) in enumerate(small)
    ]
    right_copy = pltpu.make_async_copy(right_hbm, right_ref, input_sems.at[len(small)])
    left_copy = pltpu.make_async_copy(left_hbm, left_ref, input_sems.at[len(small) + 1])
    chunk = slots // CHUNKS
    tile_copies = [
        pltpu.make_async_copy(
            tiles_hbm.at[pl.ds(i * chunk, chunk)], tiles.at[pl.ds(i * chunk, chunk)], tile_sems.at[i]
        )
        for i in range(CHUNKS)
    ]
    for copy in small_copies + [right_copy, left_copy] + tile_copies:
        copy.start()

    phases = [0]

    def next_phase():
        phases[0] += 1
        return phases[0] - 1

    pending = []

    def send_all(source, buf):
        phase = next_phase()

        def send(row, col):
            pltpu.make_async_remote_copy(
                src_ref=source(row * n_col + col), dst_ref=buf.at[me],
                send_sem=send_sems.at[phase], recv_sem=recv_sems.at[phase],
                device_id={"row": row, "col": col}, device_id_type=MESH,
            ).start()

        each_peer(send)
        many = buf.at[pl.ds(0, devices - 1)]
        pending.append((many, phase))
        return lambda: pltpu.make_async_copy(many, many, recv_sems.at[phase]).wait()

    def send_col(source, buf):
        phase = next_phase()
        for col in other_cols:
            pltpu.make_async_remote_copy(
                src_ref=source(col), dst_ref=buf.at[my_col],
                send_sem=send_sems.at[phase], recv_sem=recv_sems.at[phase],
                device_id={"row": my_row, "col": col}, device_id_type=MESH,
            ).start()
        many = buf.at[pl.ds(0, n_col - 1)]
        pending.append((many, phase))
        return lambda: pltpu.make_async_copy(many, many, recv_sems.at[phase]).wait()

    def partial_coeffs(basis, x_ref, buf):
        total = jnp.zeros((basis_rows, size), F32)
        for k in range(per_owner):
            total = total + basis[:, k * size:(k + 1) * size] * x_ref[k:k + 1, :]
        value = x_ref[...]
        acc_ref[0:basis_rows, :] = total
        acc_ref[basis_rows:basis_rows + 1, :] = jnp.sum(value * value, axis=0, keepdims=True)
        buf[me] = jnp.sum(acc_ref[...].T, axis=0, keepdims=True)

    def remainder(basis, x_ref, out_ref, line):
        column = jnp.broadcast_to(line / row_total, (size, size)).T
        for k in range(per_owner):
            part = jnp.sum(
                basis[:, k * size:(k + 1) * size] * column[0:basis_rows, :], axis=0, keepdims=True
            )
            out_ref[k:k + 1, :] = x_ref[k:k + 1, :] - part
        return column

    def gram_norm(line, column, which):
        blocks = size // gram_rows
        gram = jnp.concatenate(
            [gram_all[which * blocks + i] for i in range(blocks)], axis=0
        )
        weighted = jnp.sum(gram * column, axis=0, keepdims=True)
        lane = lax.broadcasted_iota(jnp.int32, (1, size), 1)
        terms = jnp.where(
            lane < basis_rows,
            line / row_total * (weighted - 2.0 * line),
            jnp.where(lane == basis_rows, line, 0.0),
        )
        total = jnp.maximum(jnp.sum(terms, axis=1, keepdims=True), 0.0)
        return jnp.sqrt(total / row_total + 1e-06)

    def put_coeff(i, value):
        coeffs_ref[i:i + 1, :] = jnp.broadcast_to(value, (1, size))

    def put_rows(ref, row, value):
        for k in range(per_owner):
            ref[row:row + 1, k * size:(k + 1) * size] = value[k:k + 1, :]

    def local_gram(basis, which):
        step = 4 * size

        def split(i, _):
            lanes = pl.ds(pl.multiple_of(i * step, step), step)
            value = basis[:, lanes]
            high = value.astype(BF16)
            halves[0:basis_rows, lanes] = high
            halves[size:size + basis_rows, lanes] = (value - high.astype(F32)).astype(BF16)
            return 0

        lax.fori_loop(0, basis.shape[1] // step, split, 0)
        both = lax.dot_general(
            halves[...], halves[...], (((1,), (1,)), ((), ())), preferred_element_type=F32
        )
        top, bottom = both[0:size, :], both[size:2 * size, :]
        gram = top[:, 0:size] + (
            (top[:, size:2 * size] + bottom[:, 0:size]) + bottom[:, size:2 * size]
        )
        blocks = size // gram_rows
        for i in range(blocks):
            gram_out[which * blocks + i] = gram[i * gram_rows:(i + 1) * gram_rows, :]

    def flip(part):
        tile_copies[part].wait()

        def step(i, _):
            first = part * chunk + i * 8
            for h in range(8):
                flipped[first + h] = tiles[first + h].T
            return 0

        lax.fori_loop(0, chunk // 8, step, 0)

    acc_ref[...] = jnp.zeros_like(acc_ref)
    for copy in small_copies + [right_copy]:
        copy.wait()
    partial_coeffs(right_ref, start_ref, c_buf.at[0])

    def upright(line):
        return jnp.broadcast_to(line.astype(F32), (size, slots)).T

    live_line = jnp.where(
        lax.broadcasted_iota(jnp.int32, (1, slots), 1) < counts_ref[0], row_line[...], -1
    )
    live_column = upright(live_line)[:, 0:1]
    columns = upright(col_line[...])[:, 0:1].astype(jnp.int32)
    owner = lax.div(columns, per_owner)
    place = lax.rem(columns, per_owner)
    owner_hot = hot(owner == lax.broadcasted_iota(jnp.int32, (slots, devices), 1))
    place_here = place == lax.broadcasted_iota(jnp.int32, (slots, size), 1)
    named = lax.dot_general(
        owner_hot, hot(place_here), (((0,), (0,)), ((), ())), preferred_element_type=F32
    )
    touched = named > 0.5
    earlier = hot(
        lax.broadcasted_iota(jnp.int32, (size, size), 0)
        <= lax.broadcasted_iota(jnp.int32, (size, size), 1)
    )
    rank = jnp.where(touched, dot(hot(touched), earlier) - 1.0, -1.0)
    for i in range(devices):
        place_out[i] = rank[i:i + 1, :]
    place_buf[me] = place_out[me]

    pl.semaphore_wait(barrier, devices - 1)
    coeffs_in = send_all(lambda target: c_buf.at[0, me], c_buf.at[0])
    places_in = send_all(lambda target: place_out.at[target], place_buf)

    slot_rank = jnp.sum(
        jnp.where(place_here, dot(owner_hot, rank.astype(BF16)), 0.0), axis=1, keepdims=True
    )
    entry = owner.astype(F32) * PEER_TILES + slot_rank
    entry_hot = hot(entry == lax.broadcasted_iota(jnp.int32, (slots, table), 1).astype(F32))
    entry_line = jnp.broadcast_to(entry, (slots, size)).T[0:1, :]
    entry_hot_t = hot(entry_line == lax.broadcasted_iota(jnp.int32, (table, slots), 0).astype(F32))
    row_hot = hot(
        live_column == lax.broadcasted_iota(jnp.int32, (slots, group_tiles), 1).astype(F32)
    )
    row_hot_t = hot(live_line == lax.broadcasted_iota(jnp.int32, (group_tiles, slots), 0))

    halves[...] = jnp.zeros_like(halves)
    local_gram(right_ref, 0)
    left_copy.wait()
    local_gram(left_ref, 1)
    gram_parts_in = send_all(lambda target: gram_out.at[target], gram_in)
    gram_in[me] = gram_out[me]
    for part in range(EARLY):
        flip(part)

    places_in()
    spread = hot(
        lax.div(lax.broadcasted_iota(jnp.int32, (table, devices), 0), PEER_TILES)
        == lax.broadcasted_iota(jnp.int32, (table, devices), 1)
    )
    ranks = jnp.concatenate([place_buf[i] for i in range(devices)], axis=0).astype(BF16)
    wanted = lax.rem(lax.broadcasted_iota(jnp.int32, (table, size), 0), PEER_TILES).astype(F32)
    selector_all = jnp.where(dot(spread, ranks) == wanted, 1.0, 0.0)
    selector = selector_all[:, 0:per_owner].astype(BF16)
    selector_t = selector_all.T[0:per_owner, :].astype(BF16)

    def diagonal(wide):
        index = lax.broadcasted_iota(jnp.int32, (GROUP, size), 0)
        total = wide[:, 0:size]
        for k in range(1, GROUP):
            total = jnp.where(index == k, wide[:, k * size:(k + 1) * size], total)
        return total

    def tile_products(source):
        def one(first):
            vectors = x_gathered[pl.ds(first, GROUP), :]
            block = source[pl.ds(first, GROUP)]
            joined = jnp.concatenate([block[k] for k in range(GROUP)], axis=1)
            return diagonal(dot(vectors, joined))

        def step(g, _):
            firsts = [
                pl.multiple_of(g * (GROUP * UNROLL) + h * GROUP, GROUP) for h in range(UNROLL)
            ]
            found = [one(first) for first in firsts]
            for first, value in zip(firsts, found):
                products[pl.ds(first, GROUP), :] = value
            return 0

        lax.fori_loop(0, slots // (GROUP * UNROLL), step, 0)

    def rows_product(index, values):
        x_gathered[...] = dot(entry_hot, values).astype(BF16)
        tile_products(flipped)
        ypart[index] = exact_dot(row_hot_t, products[...]).reshape(n_col, per_owner, size)
        rows_in = send_col(lambda target: ypart.at[index, target], rsbuf.at[index])
        rsbuf[index, my_col] = ypart[index, my_col]
        rows_in()
        total = rsbuf[index, 0]
        for i in range(1, n_col):
            total = total + rsbuf[index, i]
        return total

    def columns_product(index):
        values = agbuf[index].reshape(group_tiles, size)
        x_gathered[...] = dot(row_hot, values).astype(BF16)
        tile_products(tiles)
        outgoing[index] = exact_dot(entry_hot_t, products[...]).reshape(devices, PEER_TILES, size)
        sums_in = send_all(lambda target: outgoing.at[index, target], abuf.at[index])
        abuf[index, me] = outgoing[index, me]
        sums_in()
        return exact_dot(selector_t, abuf[index].reshape(table, size))

    def orthogonalize(basis, which, x_ref, out_ref, index):
        partial_coeffs(basis, x_ref, c_buf.at[index])
        send_all(lambda target: c_buf.at[index, me], c_buf.at[index])()
        line = jnp.sum(c_buf[index], axis=0)
        column = remainder(basis, x_ref, out_ref, line)
        norm = gram_norm(line, column, which)
        put_coeff(index, norm)
        return norm, out_ref[...] / norm

    scratch = r_ref
    coeffs_in()
    remainder(right_ref, start_ref, scratch.at[1], jnp.sum(c_buf[0], axis=0))
    value = scratch[1]
    n_buf[me] = jnp.sum(value * value, axis=0, keepdims=True)
    norms_in = send_all(lambda target: n_buf.at[me], n_buf)
    pack_first[...] = exact_dot(selector, value).reshape(devices, PEER_TILES, size)
    values_in = send_all(lambda target: pack_first.at[target], x_first)
    x_first[me] = pack_first[me]
    for part in range(EARLY, CHUNKS):
        flip(part)
    gram_parts_in()
    gram_total = gram_in[0]
    for i in range(1, devices):
        gram_total = gram_total + gram_in[i]
    gram_all[me] = gram_total
    norms_in()
    norm = jnp.sqrt(
        jnp.sum(jnp.sum(n_buf[...], axis=0), axis=1, keepdims=True) / row_total + 1e-06
    )
    put_coeff(0, norm)
    right_one[...] = scratch[1] / norm
    values_in()
    gram_in_all = send_all(lambda target: gram_all.at[me], gram_all)

    scratch[0] = rows_product(0, (x_first[...].reshape(table, size) / norm).astype(BF16))
    for index in range(2):
        if index == 0:
            gram_in_all()
        norm, value = orthogonalize(left_ref, 1, scratch.at[0], scratch.at[1], 2 * index + 1)
        share[index] = value.astype(BF16)
        values_in = send_col(lambda target: share.at[index], agbuf.at[index])
        agbuf[index, my_col] = share[index]
        left_one[...] = value
        put_rows(lefts_ref, index, left_one)
        values_in()
        scratch[0] = columns_product(index) - norm * right_one[...]

        norm, value = orthogonalize(right_ref, 0, scratch.at[0], scratch.at[1], 2 * index + 2)
        if index == 0:
            packed = dot(selector, value.astype(BF16)).reshape(devices, PEER_TILES, size)
            pack[...] = packed.astype(BF16)
            values_in = send_all(lambda target: pack.at[target], xbuf)
            xbuf[me] = pack[me]
        right_one[...] = value
        put_rows(rights_ref, index, right_one)
        if index == 0:
            values_in()
            found = xbuf[...].astype(F32).reshape(table, size).astype(BF16)
            scratch[0] = rows_product(1, found) - norm * left_one[...]

    for many, phase in pending:
        pltpu.make_async_copy(many, many, send_sems.at[phase]).wait()


def finish(lefts_in, rights_in, coeffs_in, lefts, rights, line):
    lefts[...] = lefts_in[...]
    rights[...] = rights_in[...]
    for i in range(5):
        line[i] = coeffs_in[i, 0]


def shards(tiles, row_tiles, col_tiles, counts, right_basis, left_basis, start):
    n_row, n_col = lax.axis_size("row"), lax.axis_size("col")
    devices = n_row * n_col
    slots, size = tiles.shape[0], tiles.shape[1]
    rows_dev = start.shape[0]
    per_owner = rows_dev // size
    row_total = float(rows_dev * devices)
    vmem = pl.BlockSpec(memory_space=pltpu.VMEM)
    hbm = pl.BlockSpec(memory_space=pl.ANY)
    n_phases = 17
    gram_rows = 2 * size // devices
    lefts, rights, coeffs = pl.pallas_call(
        functools.partial(kernel, n_row, n_col, row_total),
        out_shape=(
            jax.ShapeDtypeStruct((2, rows_dev), F32),
            jax.ShapeDtypeStruct((2, rows_dev), F32),
            jax.ShapeDtypeStruct((8, size), F32),
        ),
        in_specs=[hbm] * 7,
        out_specs=(vmem, vmem, vmem),
        scratch_shapes=[
            pltpu.VMEM(tiles.shape, BF16),
            pltpu.VMEM(tiles.shape, BF16),
            pltpu.VMEM(left_basis.shape, F32),
            pltpu.VMEM(right_basis.shape, F32),
            pltpu.VMEM((1, slots), jnp.int32),
            pltpu.VMEM((1, slots), jnp.int32),
            pltpu.SMEM((1,), jnp.int32),
            pltpu.VMEM((per_owner, size), F32),
            pltpu.VMEM((devices, 1, size), F32),
            pltpu.VMEM((devices, 1, size), F32),
            pltpu.VMEM((5, devices, 1, size), F32),
            pltpu.VMEM((devices, 1, size), F32),
            pltpu.VMEM((devices, PEER_TILES, size), F32),
            pltpu.VMEM((devices, PEER_TILES, size), F32),
            pltpu.VMEM((devices, PEER_TILES, size), BF16),
            pltpu.VMEM((devices, PEER_TILES, size), BF16),
            pltpu.VMEM((2, devices, PEER_TILES, size), F32),
            pltpu.VMEM((2, devices, PEER_TILES, size), F32),
            pltpu.VMEM((2, n_col, per_owner, size), F32),
            pltpu.VMEM((2, n_col, per_owner, size), F32),
            pltpu.VMEM((2, per_owner, size), BF16),
            pltpu.VMEM((2, n_col, per_owner, size), BF16),
            pltpu.VMEM((2 * size, rows_dev), BF16),
            pltpu.VMEM((devices, gram_rows, size), F32),
            pltpu.VMEM((devices, gram_rows, size), F32),
            pltpu.VMEM((devices, gram_rows, size), F32),
            pltpu.VMEM((2, per_owner, size), F32),
            pltpu.VMEM((per_owner, size), F32),
            pltpu.VMEM((per_owner, size), F32),
            pltpu.VMEM((size, size), F32),
            pltpu.VMEM((slots, size), BF16),
            pltpu.VMEM((slots, size), F32),
            pltpu.SemaphoreType.DMA((CHUNKS,)),
            pltpu.SemaphoreType.DMA((6,)),
            pltpu.SemaphoreType.DMA((n_phases,)),
            pltpu.SemaphoreType.DMA((n_phases,)),
        ],
        compiler_params=pltpu.CompilerParams(
            collective_id=0, has_side_effects=True, vmem_limit_bytes=60 * 1024 * 1024
        ),
    )(
        tiles, row_tiles.reshape(1, slots), col_tiles.reshape(1, slots), counts, right_basis, left_basis, start.reshape(per_owner, size),
    )
    lefts, rights, line = pl.pallas_call(
        finish,
        out_shape=(
            jax.ShapeDtypeStruct(lefts.shape, F32),
            jax.ShapeDtypeStruct(rights.shape, F32),
            jax.ShapeDtypeStruct((5,), F32),
        ),
        in_specs=[vmem, vmem, pl.BlockSpec(memory_space=pltpu.SMEM)],
        out_specs=(vmem, vmem, pl.BlockSpec(memory_space=pltpu.SMEM)),
    )(lefts, rights, coeffs)
    return lefts, rights, line


def solution(mesh):
    placed = (
        P(("row", "col"), None, None),
        P(("row", "col")),
        P(("row", "col")),
        P(("row", "col")),
        P(None, ("row", "col")),
        P(None, ("row", "col")),
        P(("row", "col")),
    )
    return jax.shard_map(
        shards,
        mesh=mesh,
        in_specs=placed,
        out_specs=(P(None, ("row", "col")), P(None, ("row", "col")), P()),
        check_vma=False,
    )
```

time: 98.6 us -> 88.6 us (0.90)
  Pallas kernels: 97.1 us -> 86.9 us
    pallas_call x1, Pallas kernels: 95.6 us -> 85.5 us  [shards(): pl.pallas_call(functools.partial(kernel, n_row, n_col, row_total), out_sh...]
where the time goes in v1:
time: 88.6 us; the launch traced here: 88.4 us
  Pallas kernels  86.9 us (98%)
  between operations  1.45 us (2%)
    pallas_call x1, Pallas kernels, shards(): pl.pallas_call(functools.partial(kernel, n_row, n_col, row_total), out_sh...  85.5 us

profile of v1, /device:TPU:0, one launch (start us, length us, event | category | flops | bytes accessed | tf_op | source)
XLA Modules:
  0.0 88.4 jit_solution(4637857768237893390)
XLA Ops:
  1.3 85.5 %shard_map.94 = (f32[2,4096]{1,0:T(2,128)}, f32[2,4096]{1,0:T(2,128)}, f32[8,128]{1,0:T(8,128)}) custom-call(bf16[512,128,128]{2,1,0:T(8,128)(2,1)} %tiles_hbm.1, s32[1,512]{1,0:T(1,128)} %bitcast.4, s32[1,512]{1,0:T(1,128)} %bitcast.5, s32[1]{0:T(128)S(6)} %copy.10.counts_hbm, f32[100,4096]{1,0:T(8,128)} %right_hbm.1, f32[100,4096]{1,0:T(8,128)} %left_hbm.1, ...), custom_call_target="tpu_custom_call" | custom-call | tf_op jit(solution)/shard_map/pallas_call | solution.py:406
  86.7 1.5 %shard_map.95 = (f32[2,4096]{1,0:T(2,128)}, f32[2,4096]{1,0:T(2,128)}, f32[5]{0:T(128)}) custom-call(f32[2,4096]{1,0:T(2,128)} %get-tuple-element.6.lefts_in, f32[2,4096]{1,0:T(2,128)} %get-tuple-element.7.rights_in, f32[8,128]{1,0:T(8,128)} %get-tuple-element.8.coeffs_in), custom_call_target="tpu_custom_call" | custom-call | tf_op jit(solution)/shard_map/pallas_call | solution.py:459

commit v2 on v1

--- a/solution.py
+++ b/solution.py
@@ -9,9 +9,10 @@
 
 PEER_TILES = 8
 GROUP = 16
-UNROLL = 32
-CHUNKS = 8
-EARLY = 2
+UNROLL = 16
+CHUNKS = 16
+DEPTH = 4
+EARLY = 4
 MESH = pl.DeviceIdType.MESH
 F32 = jnp.float32
 BF16 = jnp.bfloat16
@@ -52,7 +53,7 @@
     group_tiles = per_owner * n_col
     table = devices * PEER_TILES
     basis_rows = right_ref.shape[0]
-    gram_rows = gram_out.shape[1]
+    gram_rows = gram_out.shape[2]
 
     barrier = pltpu.get_barrier_semaphore()
 
@@ -96,7 +97,7 @@
         )
         for i in range(CHUNKS)
     ]
-    for copy in small_copies + [right_copy, left_copy] + tile_copies:
+    for copy in [right_copy] + small_copies:
         copy.start()
 
     phases = [0]
@@ -153,10 +154,7 @@
         return column
 
     def gram_norm(line, column, which):
-        blocks = size // gram_rows
-        gram = jnp.concatenate(
-            [gram_all[which * blocks + i] for i in range(blocks)], axis=0
-        )
+        gram = jnp.concatenate([gram_all[which, i] for i in range(devices)], axis=0)
         weighted = jnp.sum(gram * column, axis=0, keepdims=True)
         lane = lax.broadcasted_iota(jnp.int32, (1, size), 1)
         terms = jnp.where(
@@ -193,25 +191,32 @@
         gram = top[:, 0:size] + (
             (top[:, size:2 * size] + bottom[:, 0:size]) + bottom[:, size:2 * size]
         )
-        blocks = size // gram_rows
-        for i in range(blocks):
-            gram_out[which * blocks + i] = gram[i * gram_rows:(i + 1) * gram_rows, :]
+        for i in range(devices):
+            gram_out[which, i] = gram[i * gram_rows:(i + 1) * gram_rows, :]
+
+    def share_gram_parts(which):
+        gram_in[which, me] = gram_out[which, me]
+        return send_all(lambda target: gram_out.at[which, target], gram_in.at[which])
+
+    def share_gram_sums(which):
+        total = gram_in[which, 0]
+        for i in range(1, devices):
+            total = total + gram_in[which, i]
+        gram_all[which, me] = total
+        return send_all(lambda target: gram_all.at[which, me], gram_all.at[which])
 
     def flip(part):
         tile_copies[part].wait()
-
-        def step(i, _):
-            first = part * chunk + i * 8
-            for h in range(8):
-                flipped[first + h] = tiles[first + h].T
-            return 0
-
-        lax.fori_loop(0, chunk // 8, step, 0)
+        if part + DEPTH < CHUNKS:
+            tile_copies[part + DEPTH].start()
+        first = part * chunk
+        found = [tiles[first + h].T for h in range(chunk)]
+        for h in range(chunk):
+            flipped[first + h] = found[h]
 
     acc_ref[...] = jnp.zeros_like(acc_ref)
-    for copy in small_copies + [right_copy]:
+    for copy in small_copies:
         copy.wait()
-    partial_coeffs(right_ref, start_ref, c_buf.at[0])
 
     def upright(line):
         return jnp.broadcast_to(line.astype(F32), (size, slots)).T
@@ -238,6 +243,10 @@
         place_out[i] = rank[i:i + 1, :]
     place_buf[me] = place_out[me]
 
+    right_copy.wait()
+    for copy in [left_copy] + tile_copies[0:DEPTH]:
+        copy.start()
+    partial_coeffs(right_ref, start_ref, c_buf.at[0])
     pl.semaphore_wait(barrier, devices - 1)
     coeffs_in = send_all(lambda target: c_buf.at[0, me], c_buf.at[0])
     places_in = send_all(lambda target: place_out.at[target], place_buf)
@@ -255,11 +264,9 @@
     row_hot_t = hot(live_line == lax.broadcasted_iota(jnp.int32, (group_tiles, slots), 0))
 
     halves[...] = jnp.zeros_like(halves)
-    local_gram(right_ref, 0)
     left_copy.wait()
     local_gram(left_ref, 1)
-    gram_parts_in = send_all(lambda target: gram_out.at[target], gram_in)
-    gram_in[me] = gram_out[me]
+    left_gram_in = share_gram_parts(1)
     for part in range(EARLY):
         flip(part)
 
@@ -299,12 +306,13 @@
 
         lax.fori_loop(0, slots // (GROUP * UNROLL), step, 0)
 
-    def rows_product(index, values):
+    def rows_product(index, values, meanwhile=lambda: None):
         x_gathered[...] = dot(entry_hot, values).astype(BF16)
         tile_products(flipped)
         ypart[index] = exact_dot(row_hot_t, products[...]).reshape(n_col, per_owner, size)
         rows_in = send_col(lambda target: ypart.at[index, target], rsbuf.at[index])
         rsbuf[index, my_col] = ypart[index, my_col]
+        meanwhile()
         rows_in()
         total = rsbuf[index, 0]
         for i in range(1, n_col):
@@ -321,9 +329,11 @@
         sums_in()
         return exact_dot(selector_t, abuf[index].reshape(table, size))
 
-    def orthogonalize(basis, which, x_ref, out_ref, index):
+    def orthogonalize(basis, which, x_ref, out_ref, index, meanwhile=lambda: None):
         partial_coeffs(basis, x_ref, c_buf.at[index])
-        send_all(lambda target: c_buf.at[index, me], c_buf.at[index])()
+        coeffs_in = send_all(lambda target: c_buf.at[index, me], c_buf.at[index])
+        meanwhile()
+        coeffs_in()
         line = jnp.sum(c_buf[index], axis=0)
         column = remainder(basis, x_ref, out_ref, line)
         norm = gram_norm(line, column, which)
@@ -341,11 +351,8 @@
     x_first[me] = pack_first[me]
     for part in range(EARLY, CHUNKS):
         flip(part)
-    gram_parts_in()
-    gram_total = gram_in[0]
-    for i in range(1, devices):
-        gram_total = gram_total + gram_in[i]
-    gram_all[me] = gram_total
+    left_gram_in()
+    left_gram_in = share_gram_sums(1)
     norms_in()
     norm = jnp.sqrt(
         jnp.sum(jnp.sum(n_buf[...], axis=0), axis=1, keepdims=True) / row_total + 1e-06
@@ -353,21 +360,34 @@
     put_coeff(0, norm)
     right_one[...] = scratch[1] / norm
     values_in()
-    gram_in_all = send_all(lambda target: gram_all.at[me], gram_all)
-
-    scratch[0] = rows_product(0, (x_first[...].reshape(table, size) / norm).astype(BF16))
+
+    first_values = (x_first[...].reshape(table, size) / norm).astype(BF16)
+    scratch[0] = rows_product(0, first_values, lambda: local_gram(right_ref, 0))
     for index in range(2):
         if index == 0:
-            gram_in_all()
-        norm, value = orthogonalize(left_ref, 1, scratch.at[0], scratch.at[1], 2 * index + 1)
+            left_gram_in()
+        waits = []
+
+        def spread_right_gram():
+            if index == 0:
+                waits.append(share_gram_parts(0))
+
+        norm, value = orthogonalize(
+            left_ref, 1, scratch.at[0], scratch.at[1], 2 * index + 1, spread_right_gram
+        )
         share[index] = value.astype(BF16)
         values_in = send_col(lambda target: share.at[index], agbuf.at[index])
         agbuf[index, my_col] = share[index]
         left_one[...] = value
         put_rows(lefts_ref, index, left_one)
+        if index == 0:
+            waits[0]()
+            waits.append(share_gram_sums(0))
         values_in()
         scratch[0] = columns_product(index) - norm * right_one[...]
 
+        if index == 0:
+            waits[1]()
         norm, value = orthogonalize(right_ref, 0, scratch.at[0], scratch.at[1], 2 * index + 2)
         if index == 0:
             packed = dot(selector, value.astype(BF16)).reshape(devices, PEER_TILES, size)
@@ -401,8 +421,8 @@
     row_total = float(rows_dev * devices)
     vmem = pl.BlockSpec(memory_space=pltpu.VMEM)
     hbm = pl.BlockSpec(memory_space=pl.ANY)
-    n_phases = 17
-    gram_rows = 2 * size // devices
+    n_phases = 19
+    gram_rows = size // devices
     lefts, rights, coeffs = pl.pallas_call(
         functools.partial(kernel, n_row, n_col, row_total),
         out_shape=(
@@ -436,9 +456,9 @@
             pltpu.VMEM((2, per_owner, size), BF16),
             pltpu.VMEM((2, n_col, per_owner, size), BF16),
             pltpu.VMEM((2 * size, rows_dev), BF16),
-            pltpu.VMEM((devices, gram_rows, size), F32),
-            pltpu.VMEM((devices, gram_rows, size), F32),
-            pltpu.VMEM((devices, gram_rows, size), F32),
+            pltpu.VMEM((2, devices, gram_rows, size), F32),
+            pltpu.VMEM((2, devices, gram_rows, size), F32),
+            pltpu.VMEM((2, devices, gram_rows, size), F32),
             pltpu.VMEM((2, per_owner, size), F32),
             pltpu.VMEM((per_owner, size), F32),
             pltpu.VMEM((per_owner, size), F32),

time: 88.6 us -> 83.1 us (0.938)
  Pallas kernels: 86.9 us -> 81.5 us
    pallas_call x1, Pallas kernels: 85.5 us -> 80 us  [shards(): pl.pallas_call(functools.partial(kernel, n_row, n_col, row_total), out_sh...]
where the time goes in v2:
time: 83.1 us; the launch traced here: 82.9 us
  Pallas kernels  81.5 us (98%)
  between operations  1.45 us (2%)
    pallas_call x1, Pallas kernels, shards(): pl.pallas_call(functools.partial(kernel, n_row, n_col, row_total), out_sh...  80 us

profile of v2, /device:TPU:0, one launch (start us, length us, event | category | flops | bytes accessed | tf_op | source)
XLA Modules:
  0.0 82.9 jit_solution(1571969037571862426)
XLA Ops:
  1.3 80.0 %shard_map.94 = (f32[2,4096]{1,0:T(2,128)}, f32[2,4096]{1,0:T(2,128)}, f32[8,128]{1,0:T(8,128)}) custom-call(bf16[512,128,128]{2,1,0:T(8,128)(2,1)} %tiles_hbm.1, s32[1,512]{1,0:T(1,128)} %bitcast.4, s32[1,512]{1,0:T(1,128)} %bitcast.5, s32[1]{0:T(128)S(6)} %copy.10.counts_hbm, f32[100,4096]{1,0:T(8,128)} %right_hbm.1, f32[100,4096]{1,0:T(8,128)} %left_hbm.1, ...), custom_call_target="tpu_custom_call" | custom-call | tf_op jit(solution)/shard_map/pallas_call | solution.py:426
  81.2 1.5 %shard_map.95 = (f32[2,4096]{1,0:T(2,128)}, f32[2,4096]{1,0:T(2,128)}, f32[5]{0:T(128)}) custom-call(f32[2,4096]{1,0:T(2,128)} %get-tuple-element.6.lefts_in, f32[2,4096]{1,0:T(2,128)} %get-tuple-element.7.rights_in, f32[8,128]{1,0:T(8,128)} %get-tuple-element.8.coeffs_in), custom_call_target="tpu_custom_call" | custom-call | tf_op jit(solution)/shard_map/pallas_call | solution.py:479

commit v3 on v2

--- a/solution.py
+++ b/solution.py
@@ -118,7 +118,11 @@
                 device_id={"row": row, "col": col}, device_id_type=MESH,
             ).start()
 
-        each_peer(send)
+        for col in other_cols:
+            for i in range(n_row - 1, -1, -1):
+                send(lax.rem(my_row + i, n_row), col)
+        for i in range(n_row - 1, 0, -1):
+            send(lax.rem(my_row + i, n_row), my_col)
         many = buf.at[pl.ds(0, devices - 1)]
         pending.append((many, phase))
         return lambda: pltpu.make_async_copy(many, many, recv_sems.at[phase]).wait()
@@ -166,7 +170,9 @@
         return jnp.sqrt(total / row_total + 1e-06)
 
     def put_coeff(i, value):
-        coeffs_ref[i:i + 1, :] = jnp.broadcast_to(value, (1, size))
+        lane = lax.broadcasted_iota(jnp.int32, (1, size), 1)
+        line = jnp.broadcast_to(value, (1, size))
+        coeffs_ref[...] = line if i == 0 else jnp.where(lane == i, line, coeffs_ref[...])
 
     def put_rows(ref, row, value):
         for k in range(per_owner):
@@ -408,8 +414,7 @@
 def finish(lefts_in, rights_in, coeffs_in, lefts, rights, line):
     lefts[...] = lefts_in[...]
     rights[...] = rights_in[...]
-    for i in range(5):
-        line[i] = coeffs_in[i, 0]
+    line[...] = coeffs_in[0, 0:line.shape[0]]
 
 
 def shards(tiles, row_tiles, col_tiles, counts, right_basis, left_basis, start):
@@ -428,7 +433,7 @@
         out_shape=(
             jax.ShapeDtypeStruct((2, rows_dev), F32),
             jax.ShapeDtypeStruct((2, rows_dev), F32),
-            jax.ShapeDtypeStruct((8, size), F32),
+            jax.ShapeDtypeStruct((1, size), F32),
         ),
         in_specs=[hbm] * 7,
         out_specs=(vmem, vmem, vmem),
@@ -483,8 +488,8 @@
             jax.ShapeDtypeStruct(rights.shape, F32),
             jax.ShapeDtypeStruct((5,), F32),
         ),
-        in_specs=[vmem, vmem, pl.BlockSpec(memory_space=pltpu.SMEM)],
-        out_specs=(vmem, vmem, pl.BlockSpec(memory_space=pltpu.SMEM)),
+        in_specs=[vmem] * 3,
+        out_specs=(vmem,) * 3,
     )(lefts, rights, coeffs)
     return lefts, rights, line
 

time: 83.1 us -> 81.5 us (0.981)
  Pallas kernels: 81.5 us -> 80 us
    pallas_call x1, Pallas kernels: 80 us -> 78.6 us  [shards(): pl.pallas_call(functools.partial(kernel, n_row, n_col, row_total), out_sh...]
where the time goes in v3:
time: 81.5 us; the launch traced here: 81.3 us
  Pallas kernels  80 us (98%)
  between operations  1.29 us (2%)
    pallas_call x1, Pallas kernels, shards(): pl.pallas_call(functools.partial(kernel, n_row, n_col, row_total), out_sh...  78.6 us

profile of v3, /device:TPU:0, one launch (start us, length us, event | category | flops | bytes accessed | tf_op | source)
XLA Modules:
  0.0 81.3 jit_solution(15694070723570331829)
XLA Ops:
  1.3 78.6 %shard_map.94 = (f32[2,4096]{1,0:T(2,128)}, f32[2,4096]{1,0:T(2,128)}, f32[1,128]{1,0:T(1,128)}) custom-call(bf16[512,128,128]{2,1,0:T(8,128)(2,1)} %tiles_hbm.1, s32[1,512]{1,0:T(1,128)} %bitcast.4, s32[1,512]{1,0:T(1,128)} %bitcast.5, s32[1]{0:T(128)S(6)} %copy.10.counts_hbm, f32[100,4096]{1,0:T(8,128)} %right_hbm.1, f32[100,4096]{1,0:T(8,128)} %left_hbm.1, ...), custom_call_target="tpu_custom_call" | custom-call | tf_op jit(solution)/shard_map/pallas_call | solution.py:431
  79.9 1.4 %shard_map.95 = (f32[2,4096]{1,0:T(2,128)}, f32[2,4096]{1,0:T(2,128)}, f32[5]{0:T(128)}) custom-call(f32[2,4096]{1,0:T(2,128)} %get-tuple-element.6.lefts_in, f32[2,4096]{1,0:T(2,128)} %get-tuple-element.7.rights_in, f32[1,128]{1,0:T(1,128)} %get-tuple-element.8.coeffs_in), custom_call_target="tpu_custom_call" | custom-call | tf_op jit(solution)/shard_map/pallas_call | solution.py:484
